TPU v7x, 32 devices: a whole 2x2x4 slice. The times are simulated.
32 devices in a mesh: space: 16 (over z, y, x), level: 2 (over core).
Axes of the slice: x: 2, y: 2, z: 4, core: 2. Of those that a mesh axis runs over, the one named last changes fastest.
Arguments:
- velocity: float32 [2, 16, 16384], P(None, 'level', 'space'), may hold values from -3 to 3
- density: float32 [16, 16384], P('level', 'space'), may hold values from -6 to 6
- elevation: float32 [16384], P('space'), may hold values from -3 to 3
- grad_weights: float32 [2, 6, 16384], P(None, None, 'space'), may hold values from -2.4 to 2.4
- lap_weights: float32 [6, 16384], P(None, 'space'), may hold values from 0.02 to 0.2
- coriolis: float32 [16384], P('space'), may hold values from 0.5 to 2
- node_area: float32 [16384], P('space'), may hold values from 1 to 100, as said below
- thickness: float32 [16], P('level'), may hold values from 0.5 to 2
- send_list: int32 [16, 256], P('space'), may hold values from 0 to 1023
- neighbours: int32 [6, 16384], P(None, 'space'), may hold values from 0 to 1279
- bottom: int32 [16384], P('space'), may hold values from 0 to 16, as said below
Outputs:
- velocity_out: float32 [2, 16, 16384], P(None, 'level', 'space')
- density_out: float32 [16, 16384], P('level', 'space')
- elevation_out: float32 [16384], P('space')
- volume_drift: float32 [4], replicated
Inputs may be any that keep to these rules, and one draw needn't show every extreme that they name: `send_list`: local node numbers within the sending partition; the first 128 go to the partition one below along space, the other 128 to the one above. `neighbours`: slots below 1024 are the partition's own nodes; the next 128 are halo slots filled from the partition below, the last 128 from the partition above. Levels of a node are wet from the surface down to bottom - 1; a node with 0 is dry. Some partitions are shallower than others. `node_area`: positive areas.
All inputs are finite; a program needn't handle non-finite values.
Results may differ from a plain program's by a relative error of at most 0.00013.
Values sent between devices are 32-bit elements; how exact they have to be, the bound alone decides.
A program may use at most 64 MiB of HBM per device.

v0:
```python
import jax
import jax.numpy as jnp
from jax import lax
from jax.sharding import PartitionSpec as P

STEPS = 4


time_step = 0.1
buoyancy = 0.5
drag_rate = 0.5


def extended_2(array, sides, width):
    for axis, dim in sides:
        devices, length = (lax.axis_size(axis), array.shape[dim])
        up = [(i, (i + 1) % devices) for i in range(devices - 1)]
        down = [(j, i) for i, j in up]
        last = lax.slice_in_dim(array, length - width, length, axis=dim)
        first = lax.slice_in_dim(array, 0, width, axis=dim)
        before = lax.ppermute(last, axis, up)
        after = lax.ppermute(first, axis, down)
        array = jnp.concatenate([before, array, after], axis=dim)
    return array


def prefix(value, axis, join, neutral):
    count, mine = (lax.axis_size(axis), lax.axis_index(axis))
    pieces = lax.all_gather(value, axis)
    total = jnp.full_like(value, 0) + jnp.asarray(neutral, value.dtype)

    def hop(position, total):
        longer = join(total, pieces[position])
        return jnp.where(position < mine, longer, total)

    return lax.fori_loop(0, count - 1, hop, total)


def add_terms(earlier, later):
    return earlier + later


def neighbour_terms(fields, neighbours, weights):
    node_count = neighbours.shape[1]
    near_count = neighbours.shape[0]
    node_major = fields.T
    nearby = jnp.take(node_major, neighbours.reshape(-1), axis=0)
    nearby = nearby.reshape(near_count, node_count, fields.shape[0])
    differ = nearby - node_major[None, :node_count]
    return tuple(
        (
            jnp.einsum("knr,kn->rn", differ, weight, precision=lax.Precision.HIGHEST)
            for weight in weights
        )
    )


def local(
    velocity,
    density,
    elevation,
    grad_weights,
    lap_weights,
    coriolis,
    node_area,
    thickness,
    send_list,
    neighbours,
    bottom,
):
    level_count = density.shape[0]
    node_count = density.shape[1]
    half_slots = send_list.shape[1] // 2
    level_first = lax.axis_index("level") * level_count
    level_ids = level_first + jnp.arange(level_count, dtype=jnp.int32)
    wet_cells = (level_ids[:, None] < bottom[None, :]).astype(jnp.float32)
    at_floor = (level_ids[:, None] == bottom[None, :] - 1).astype(jnp.float32)
    wet_nodes = (bottom > 0).astype(jnp.float32)
    space_rank = lax.axis_index("space")
    space_count = lax.axis_size("space")
    slot_ids = jnp.arange(2 * half_slots, dtype=jnp.int32)
    halo_valid = jnp.where(
        slot_ids < half_slots, space_rank > 0, space_rank < space_count - 1
    ).astype(jnp.float32)
    valid_wide = jnp.concatenate([jnp.ones((node_count,), jnp.float32), halo_valid])
    valid_near = jnp.take(valid_wide, neighbours)
    weights = (grad_weights[0] * valid_near, grad_weights[1] * valid_near, lap_weights * valid_near)
    outgoing_ids = send_list[0]
    area_local = jnp.sum(node_area * wet_nodes)
    velocity = velocity * wet_cells[None]
    volume_terms = []
    for counter in range(STEPS):
        stacked = jnp.concatenate(
            [velocity.reshape(2 * level_count, node_count), density, elevation[None]], axis=0
        )
        outgoing = jnp.take(stacked.T, outgoing_ids, axis=0).T
        padded = extended_2(outgoing, (("space", 1),), half_slots)
        remote = jnp.concatenate([padded[:, :half_slots], padded[:, 3 * half_slots :]], axis=1)
        extended = jnp.concatenate([stacked, remote], axis=1)
        wide_velocity = extended[: 2 * level_count].reshape(2, level_count, extended.shape[1])
        wide_density = extended[2 * level_count : 3 * level_count]
        weighted = wide_density * thickness[:, None]
        own_total = jnp.sum(weighted, axis=0)
        transport_part = jnp.einsum(
            "cle,l->ce", wide_velocity, thickness, precision=lax.Precision.HIGHEST
        )
        above_sum = prefix(own_total, "level", add_terms, jnp.zeros_like(own_total))
        transport = lax.psum(transport_part, "level")
        pressure = buoyancy * (above_sum[None] + jnp.cumsum(weighted, axis=0) - 0.5 * weighted)
        fields = jnp.concatenate([extended, pressure, transport], axis=0)
        gradient_east, gradient_north, laplace = neighbour_terms(fields, neighbours, weights)
        elev_row = 3 * level_count
        press_first = 3 * level_count + 1
        flow_row = 4 * level_count + 1
        diverge = gradient_east[flow_row] + gradient_north[flow_row + 1]
        volume_term = jnp.sum(node_area * wet_nodes * diverge)
        new_elevation = elevation - time_step * wet_nodes * diverge
        volume_terms.append(volume_term)
        east_speed = velocity[0]
        north_speed = velocity[1]
        push_east = (
            -gradient_east[elev_row][None]
            - gradient_east[press_first : press_first + level_count]
            + coriolis[None] * north_speed
            + laplace[:level_count]
            - drag_rate * at_floor * east_speed
        )
        push_north = (
            -gradient_north[elev_row][None]
            - gradient_north[press_first : press_first + level_count]
            - coriolis[None] * east_speed
            + laplace[level_count : 2 * level_count]
            - drag_rate * at_floor * north_speed
        )
        density = density + time_step * (
            laplace[2 * level_count : 3 * level_count]
            - east_speed * gradient_east[2 * level_count : 3 * level_count]
            - north_speed * gradient_north[2 * level_count : 3 * level_count]
        )
        velocity = wet_cells[None] * (velocity + time_step * jnp.stack([push_east, push_north]))
        elevation = new_elevation
    summed, area_total = lax.psum((jnp.stack(volume_terms), area_local), "space")
    drifts = summed / area_total
    elevation = elevation + time_step * jnp.sum(drifts)
    return (velocity, density, elevation, drifts.astype(jnp.float32))


def solution(mesh):
    return jax.shard_map(
        local,
        mesh=mesh,
        in_specs=(
            P(None, "level", "space"),
            P("level", "space"),
            P("space"),
            P(None, None, "space"),
            P(None, "space"),
            P("space"),
            P("space"),
            P("level"),
            P("space", None),
            P(None, "space"),
            P("space"),
        ),
        out_specs=(P(None, "level", "space"), P("level", "space"), P("space"), P()),
        check_vma=False,
    )
```

profile of v0, /device:TPU:0, one launch (start us, length us, event | category | flops | bytes accessed | tf_op | source)
XLA Modules:
  0.0 274.5 jit_solution(15536687425961770250)
XLA Ops:
  5.5 4.9 %collective-permute-start = (f32[25,128]{0,1:T(8,128)S(1)}, f32[25,128]{0,1:T(8,128)S(1)}, u32[]{:S(2)}, u32[]{:S(2)}) collective-permute-start(f32[25,128]{0,1:T(8,128)S(1)} %get-tuple-element.135), channel_id=1, source_target_pairs={{0,2},{2,4},{4,6},{6,8},{8,10},{10,12},{12,14},{14,16},{16,18},{18... | collective-permute-start | bytes 38408 | tf_op jit(solution)/shard_map/ppermute | solution.py:21
  14.2 34.3 %gather_fusion = f32[6144]{0:T(1024)S(1)} fusion(f32[1280]{0:T(1024)S(1)} %pad_convert_fusion, s32[6144]{0:T(1024)S(1)} %broadcast_clamp_fusion), kind=kCustom, calls=%fused_computation.8 | custom fusion | bytes 73728 | tf_op jit(solution)/shard_map/jit(_take)/gather | solution.py:86
  51.0 3.3 %psum.42 = f32[2,1280]{1,0:T(2,128)S(1)} all-reduce(f32[2,1280]{1,0:T(2,128)S(1)} %bitcast.280), channel_id=1, replica_groups=mesh['space'=16,'level'=2] {'level'}, use_global_device_ids=true, to_apply=%region_2.4 | all-reduce | flops 2560 | bytes 20480 | tf_op jit(solution)/shard_map/psum | solution.py:108
  54.7 20.9 %gather_fusion.2 = f32[6144,35]{1,0:T(8,128)} fusion(f32[1280,35]{1,0:T(8,128)S(1)} %bitcast.231, s32[6144]{0:T(1024)S(1)} %fusion.68), kind=kCustom, calls=%fused_computation.1.clone | custom fusion | bytes 1744896 | tf_op jit(solution)/shard_map/jit(_take)/gather | solution.py:47
  75.6 4.7 %broadcast_select_fusion.3 = f32[6144,35]{1,0:T(8,128)S(1)} fusion(f32[6144,35]{1,0:T(8,128)} %gather_fusion.2, pred[6144]{0:T(1024)(128)(4,1)S(1)} %compare_and_fusion), kind=kLoop, calls=%fused_computation.24 | loop fusion | flops 215040 | bytes 1726464 | tf_op jit(solution)/shard_map/jit(_take)/select_n | solution.py:47
  80.3 3.2 %multiply_reduce_fusion.11 = (f32[1024,35]{1,0:T(8,128)S(1)}, f32[1024,35]{1,0:T(8,128)S(1)}, f32[1024,35]{1,0:T(8,128)S(1)}) fusion(f32[6,1024,35]{2,1,0:T(8,128)S(1)} %bitcast.237, f32[1024,6]{0,1:T(8,128)S(1)} %get-tuple-element.139, f32[1024,35]{1,0:T(8,128)S(1)} %slice.329, f32[1024,6]{0,1:T(8,128)S(1)} %get-tuple-element.138, ...), kind=kLoop, calls=%fused_computation.20 | loop fusion | flops 1397760 | bytes 1507328
  85.4 4.6 %collective-permute-start.2 = (f32[25,128]{0,1:T(8,128)S(1)}, f32[25,128]{0,1:T(8,128)S(1)}, u32[]{:S(2)}, u32[]{:S(2)}) collective-permute-start(f32[25,128]{0,1:T(8,128)S(1)} %get-tuple-element.133), channel_id=1, source_target_pairs={{0,2},{2,4},{4,6},{6,8},{8,10},{10,12},{12,14},{14,16},{16,18},{18... | collective-permute-start | bytes 38408 | tf_op jit(solution)/shard_map/ppermute | solution.py:21
  91.9 4.7 %collective-permute-done.3 = f32[25,128]{0,1:T(8,128)S(1)} collective-permute-done((f32[25,128]{0,1:T(8,128)S(1)}, f32[25,128]{0,1:T(8,128)S(1)}, u32[]{:S(2)}, u32[]{:S(2)}) %collective-permute-start.3) | collective-permute-done | bytes 12832 | tf_op jit(solution)/shard_map/ppermute | solution.py:22
  98.8 3.3 %psum.43 = f32[2,1280]{1,0:T(2,128)S(1)} all-reduce(f32[2,1280]{1,0:T(2,128)S(1)} %bitcast.281), channel_id=1, replica_groups=mesh['space'=16,'level'=2] {'level'}, use_global_device_ids=true, to_apply=%region_5.8 | all-reduce | flops 2560 | bytes 20480 | tf_op jit(solution)/shard_map/psum | solution.py:108
  102.4 20.9 %gather_fusion.4 = f32[6144,35]{1,0:T(8,128)} fusion(f32[1280,35]{1,0:T(8,128)S(1)} %bitcast.232, s32[6144]{0:T(1024)S(1)} %fusion.68), kind=kCustom, calls=%fused_computation.5.clone | custom fusion | bytes 1744896 | tf_op jit(solution)/shard_map/jit(_take)/gather | solution.py:47
  123.4 4.7 %broadcast_select_fusion.2 = f32[6144,35]{1,0:T(8,128)S(1)} fusion(f32[6144,35]{1,0:T(8,128)} %gather_fusion.4, pred[6144]{0:T(1024)(128)(4,1)S(1)} %compare_and_fusion), kind=kLoop, calls=%fused_computation.23 | loop fusion | flops 215040 | bytes 1726464 | tf_op jit(solution)/shard_map/jit(_take)/select_n | solution.py:47
  128.0 3.2 %multiply_reduce_fusion.8 = (f32[1024,35]{1,0:T(8,128)S(1)}, f32[1024,35]{1,0:T(8,128)S(1)}, f32[1024,35]{1,0:T(8,128)S(1)}) fusion(f32[6,1024,35]{2,1,0:T(8,128)S(1)} %bitcast.238, f32[1024,6]{0,1:T(8,128)S(1)} %get-tuple-element.139, f32[1024,35]{1,0:T(8,128)S(1)} %slice.346, f32[1024,6]{0,1:T(8,128)S(1)} %get-tuple-element.138, ...), kind=kLoop, calls=%fused_computation.17 | loop fusion | flops 1397760 | bytes 1507328
  133.1 4.7 %collective-permute-start.4 = (f32[25,128]{0,1:T(8,128)S(1)}, f32[25,128]{0,1:T(8,128)S(1)}, u32[]{:S(2)}, u32[]{:S(2)}) collective-permute-start(f32[25,128]{0,1:T(8,128)S(1)} %get-tuple-element.131), channel_id=1, source_target_pairs={{0,2},{2,4},{4,6},{6,8},{8,10},{10,12},{12,14},{14,16},{16,18},{18... | collective-permute-start | bytes 38408 | tf_op jit(solution)/shard_map/ppermute | solution.py:21
  139.8 4.2 %collective-permute-done.5 = f32[25,128]{0,1:T(8,128)S(1)} collective-permute-done((f32[25,128]{0,1:T(8,128)S(1)}, f32[25,128]{0,1:T(8,128)S(1)}, u32[]{:S(2)}, u32[]{:S(2)}) %collective-permute-start.5) | collective-permute-done | bytes 12832 | tf_op jit(solution)/shard_map/ppermute | solution.py:22
  146.3 3.3 %psum.44 = f32[2,1280]{1,0:T(2,128)S(1)} all-reduce(f32[2,1280]{1,0:T(2,128)S(1)} %bitcast.282), channel_id=1, replica_groups=mesh['space'=16,'level'=2] {'level'}, use_global_device_ids=true, to_apply=%region_8.11 | all-reduce | flops 2560 | bytes 20480 | tf_op jit(solution)/shard_map/psum | solution.py:108
  149.9 20.9 %gather_fusion.6 = f32[6144,35]{1,0:T(8,128)} fusion(f32[1280,35]{1,0:T(8,128)S(1)} %bitcast.234, s32[6144]{0:T(1024)S(1)} %fusion.68), kind=kCustom, calls=%fused_computation.6.clone | custom fusion | bytes 1744896 | tf_op jit(solution)/shard_map/jit(_take)/gather | solution.py:47
  170.8 4.7 %broadcast_select_fusion.1 = f32[6144,35]{1,0:T(8,128)S(1)} fusion(f32[6144,35]{1,0:T(8,128)} %gather_fusion.6, pred[6144]{0:T(1024)(128)(4,1)S(1)} %compare_and_fusion), kind=kLoop, calls=%fused_computation.22 | loop fusion | flops 215040 | bytes 1726464 | tf_op jit(solution)/shard_map/jit(_take)/select_n | solution.py:47
  175.5 3.2 %multiply_reduce_fusion.5 = (f32[1024,35]{1,0:T(8,128)S(1)}, f32[1024,35]{1,0:T(8,128)S(1)}, f32[1024,35]{1,0:T(8,128)S(1)}) fusion(f32[6,1024,35]{2,1,0:T(8,128)S(1)} %bitcast.239, f32[1024,6]{0,1:T(8,128)S(1)} %get-tuple-element.139, f32[1024,35]{1,0:T(8,128)S(1)} %slice.363, f32[1024,6]{0,1:T(8,128)S(1)} %get-tuple-element.138, ...), kind=kLoop, calls=%fused_computation.14 | loop fusion | flops 1397760 | bytes 1507328
  180.5 4.8 %collective-permute-start.6 = (f32[25,128]{0,1:T(8,128)S(1)}, f32[25,128]{0,1:T(8,128)S(1)}, u32[]{:S(2)}, u32[]{:S(2)}) collective-permute-start(f32[25,128]{0,1:T(8,128)S(1)} %get-tuple-element.129), channel_id=1, source_target_pairs={{0,2},{2,4},{4,6},{6,8},{8,10},{10,12},{12,14},{14,16},{16,18},{18... | collective-permute-start | bytes 38408 | tf_op jit(solution)/shard_map/ppermute | solution.py:21
  187.2 4.2 %collective-permute-done.7 = f32[25,128]{0,1:T(8,128)S(1)} collective-permute-done((f32[25,128]{0,1:T(8,128)S(1)}, f32[25,128]{0,1:T(8,128)S(1)}, u32[]{:S(2)}, u32[]{:S(2)}) %collective-permute-start.7) | collective-permute-done | bytes 12832 | tf_op jit(solution)/shard_map/ppermute | solution.py:22
  193.8 3.3 %psum.45 = f32[2,1280]{1,0:T(2,128)S(1)} all-reduce(f32[2,1280]{1,0:T(2,128)S(1)} %bitcast.283), channel_id=1, replica_groups=mesh['space'=16,'level'=2] {'level'}, use_global_device_ids=true, to_apply=%region_11.14 | all-reduce | flops 2560 | bytes 20480 | tf_op jit(solution)/shard_map/psum | solution.py:108
  197.3 20.9 %gather_fusion.8 = f32[6144,35]{1,0:T(8,128)} fusion(f32[1280,35]{1,0:T(8,128)S(1)} %bitcast.228, s32[6144]{0:T(1024)S(1)} %fusion.68), kind=kCustom, calls=%fused_computation.7.clone | custom fusion | bytes 1744896 | tf_op jit(solution)/shard_map/jit(_take)/gather | solution.py:47
  218.3 4.7 %broadcast_select_fusion = f32[6144,35]{1,0:T(8,128)S(1)} fusion(f32[6144,35]{1,0:T(8,128)} %gather_fusion.8, pred[6144]{0:T(1024)(128)(4,1)S(1)} %compare_and_fusion), kind=kLoop, calls=%fused_computation.21 | loop fusion | flops 215040 | bytes 1726464 | tf_op jit(solution)/shard_map/jit(_take)/select_n | solution.py:47
  230.0 40.0 %all-reduce.1 = (f32[4]{0:T(128)S(1)}, f32[]{:T(128)}) all-reduce(f32[4]{0:T(128)S(1)} %pad_maximum_fusion.36, f32[]{:T(128)} %get-tuple-element.86), channel_id=1, replica_groups=mesh['space'=16,'level'=2] {'space'}, use_global_device_ids=true, to_apply=%region_16.19 | all-reduce | flops 5 | bytes 40 | tf_op jit(solution)/shard_map/psum | solution.py:142
  (155 shorter events, 41.2 us)
Async XLA Ops:
  5.5 43.2 %collective-permute-start = (f32[25,128]{0,1:T(8,128)S(1)}, f32[25,128]{0,1:T(8,128)S(1)}, u32[]{:S(2)}, u32[]{:S(2)}) collective-permute-start(f32[25,128]{0,1:T(8,128)S(1)} %get-tuple-element.135), channel_id=1, source_target_pairs={{0,2},{2,4},{4,6},{6,8},{8,10},{10,12},{12,14},{14,16},{16,18},{18... | collective-permute-start | bytes 38408 | tf_op jit(solution)/shard_map/ppermute | solution.py:21
  10.4 38.4 %collective-permute-start.1 = (f32[25,128]{0,1:T(8,128)S(1)}, f32[25,128]{0,1:T(8,128)S(1)}, u32[]{:S(2)}, u32[]{:S(2)}) collective-permute-start(f32[25,128]{0,1:T(8,128)S(1)} %get-tuple-element.136), channel_id=1, source_target_pairs={{2,0},{4,2},{6,4},{8,6},{10,8},{12,10},{14,12},{16,14},{18,16},{20... | collective-permute-start | bytes 38408 | tf_op jit(solution)/shard_map/ppermute | solution.py:22
  14.1 34.4 %copy-start.5 = (f32[2,6,1024]{2,0,1:T(2,128)S(1)}, f32[2,6,1024]{2,0,1:T(2,128)}, u32[]{:S(2)}) copy-start(f32[2,6,1024]{2,0,1:T(2,128)} %param.18) | copy-start | bytes 147460
  14.1 34.4 %copy-start.2 = (s32[6,1024]{1,0:T(8,128)S(1)}, s32[6,1024]{1,0:T(8,128)}, u32[]{:S(2)}) copy-start(s32[6,1024]{1,0:T(8,128)} %param.24) | copy-start | bytes 73732
  14.2 34.4 %copy-start.7 = (f32[6,1024]{1,0:T(8,128)S(1)}, f32[6,1024]{1,0:T(8,128)}, u32[]{:S(2)}) copy-start(f32[6,1024]{1,0:T(8,128)} %param.19) | copy-start | bytes 73732
  14.2 34.5 %copy-start.6 = (s32[1024]{0:T(1024)S(1)}, s32[1024]{0:T(1024)}, u32[]{:S(2)}) copy-start(s32[1024]{0:T(1024)} %param.25) | copy-start | bytes 12292
  14.2 34.6 %copy-start.1 = (f32[8,1024]{1,0:T(8,128)S(1)}, f32[8,1024]{1,0:T(8,128)}, u32[]{:S(2)}) copy-start(f32[8,1024]{1,0:T(8,128)} %param.16) | copy-start | bytes 98308
  14.2 34.6 %copy-start.4 = (f32[1024]{0:T(1024)S(1)}, f32[1024]{0:T(1024)}, u32[]{:S(2)}) copy-start(f32[1024]{0:T(1024)} %param.17) | copy-start | bytes 12292
  14.2 34.6 %copy-start.8 = (f32[8]{0:T(128)S(1)}, f32[8]{0:T(128)}, u32[]{:S(2)}) copy-start(f32[8]{0:T(128)} %param.22) | copy-start | bytes 100
  80.3 3.8 %copy-start.3 = (f32[1024]{0:T(1024)S(1)}, f32[1024]{0:T(1024)}, u32[]{:S(2)}) copy-start(f32[1024]{0:T(1024)} %param.20) | copy-start | bytes 12292
  80.3 3.9 %copy-start = (f32[2,8,1024]{2,1,0:T(8,128)S(1)}, f32[2,8,1024]{2,1,0:T(8,128)}, u32[]{:S(2)}) copy-start(f32[2,8,1024]{2,1,0:T(8,128)} %param.15) | copy-start | bytes 196612
  85.4 6.4 %collective-permute-start.2 = (f32[25,128]{0,1:T(8,128)S(1)}, f32[25,128]{0,1:T(8,128)S(1)}, u32[]{:S(2)}, u32[]{:S(2)}) collective-permute-start(f32[25,128]{0,1:T(8,128)S(1)} %get-tuple-element.133), channel_id=1, source_target_pairs={{0,2},{2,4},{4,6},{6,8},{8,10},{10,12},{12,14},{14,16},{16,18},{18... | collective-permute-start | bytes 38408 | tf_op jit(solution)/shard_map/ppermute | solution.py:21
  89.9 6.6 %collective-permute-start.3 = (f32[25,128]{0,1:T(8,128)S(1)}, f32[25,128]{0,1:T(8,128)S(1)}, u32[]{:S(2)}, u32[]{:S(2)}) collective-permute-start(f32[25,128]{0,1:T(8,128)S(1)} %get-tuple-element.134), channel_id=1, source_target_pairs={{2,0},{4,2},{6,4},{8,6},{10,8},{12,10},{14,12},{16,14},{18,16},{20... | collective-permute-start | bytes 38408 | tf_op jit(solution)/shard_map/ppermute | solution.py:22
  133.1 6.6 %collective-permute-start.4 = (f32[25,128]{0,1:T(8,128)S(1)}, f32[25,128]{0,1:T(8,128)S(1)}, u32[]{:S(2)}, u32[]{:S(2)}) collective-permute-start(f32[25,128]{0,1:T(8,128)S(1)} %get-tuple-element.131), channel_id=1, source_target_pairs={{0,2},{2,4},{4,6},{6,8},{8,10},{10,12},{12,14},{14,16},{16,18},{18... | collective-permute-start | bytes 38408 | tf_op jit(solution)/shard_map/ppermute | solution.py:21
  137.8 6.2 %collective-permute-start.5 = (f32[25,128]{0,1:T(8,128)S(1)}, f32[25,128]{0,1:T(8,128)S(1)}, u32[]{:S(2)}, u32[]{:S(2)}) collective-permute-start(f32[25,128]{0,1:T(8,128)S(1)} %get-tuple-element.132), channel_id=1, source_target_pairs={{2,0},{4,2},{6,4},{8,6},{10,8},{12,10},{14,12},{16,14},{18,16},{20... | collective-permute-start | bytes 38408 | tf_op jit(solution)/shard_map/ppermute | solution.py:22
  180.5 6.6 %collective-permute-start.6 = (f32[25,128]{0,1:T(8,128)S(1)}, f32[25,128]{0,1:T(8,128)S(1)}, u32[]{:S(2)}, u32[]{:S(2)}) collective-permute-start(f32[25,128]{0,1:T(8,128)S(1)} %get-tuple-element.129), channel_id=1, source_target_pairs={{0,2},{2,4},{4,6},{6,8},{8,10},{10,12},{12,14},{14,16},{16,18},{18... | collective-permute-start | bytes 38408 | tf_op jit(solution)/shard_map/ppermute | solution.py:21
  185.3 6.2 %collective-permute-start.7 = (f32[25,128]{0,1:T(8,128)S(1)}, f32[25,128]{0,1:T(8,128)S(1)}, u32[]{:S(2)}, u32[]{:S(2)}) collective-permute-start(f32[25,128]{0,1:T(8,128)S(1)} %get-tuple-element.130), channel_id=1, source_target_pairs={{2,0},{4,2},{6,4},{8,6},{10,8},{12,10},{14,12},{16,14},{18,16},{20... | collective-permute-start | bytes 38408 | tf_op jit(solution)/shard_map/ppermute | solution.py:22
  223.0 3.6 %copy-start.9 = (f32[1024]{0:T(1024)S(1)}, f32[1024]{0:T(1024)}, u32[]{:S(2)}) copy-start(f32[1024]{0:T(1024)} %param.21) | copy-start | bytes 12292
where the time goes:
time: 276 us; the launch traced here: 275 us
  local copies, waits for them, and re-layouts  127 us (46%)
  blocking collectives  60.4 us (22%)
  other arithmetic  45.6 us (17%)
  starting transfers between devices  24.1 us (9%)
  waiting for transfers between devices  14.7 us (5%)
    gather x4, local copies, waits for them, and re-layouts, neighbour_terms(): nearby = jnp.take(node_major, neighbours.reshape(-1), axis=0)  83.6 us
    psum x1, blocking collectives, local(): lax.psum((jnp.stack(volume_terms), area_local), 'space')  40 us
    gather x2, local copies, waits for them, and re-layouts, local(): valid_near = jnp.take(valid_wide, neighbours)  34.3 us
    ppermute x4, starting transfers between devices, extended_2(): before = lax.ppermute(last, axis, up)  18.9 us
    select_n x4, other arithmetic, neighbour_terms(): nearby = jnp.take(node_major, neighbours.reshape(-1), axis=0)  18.7 us
    psum x4, blocking collectives, local(): transport = lax.psum(transport_part, 'level')  13.2 us
    ppermute x4, waiting for transfers between devices, extended_2(): after = lax.ppermute(first, axis, down)  13.1 us
    unnamed x5, other arithmetic  12.7 us
  transfers between devices with their start and end apart: 8, of which 6 were waited for; matrix products, arithmetic and copies ran while one was open for 14% of the time, Pallas kernels for 0%

commit v1 on v0

v1 whole, which is shorter than its diff:
```python
import functools

import jax
import jax.numpy as jnp
from jax import lax
from jax.experimental import pallas as pl
from jax.experimental.pallas import tpu as pltpu
from jax.sharding import PartitionSpec as P

STEPS = 4
LANES = 128

time_step = 0.1
buoyancy = 0.5
drag_rate = 0.5


def lane_gather(values, lanes):
    return jnp.take_along_axis(values, lanes, axis=1, mode="promise_in_bounds")


def pick(tiles, lanes, masks):
    found = lane_gather(tiles[0], lanes)
    for tile, mask in zip(tiles[1:], masks):
        found = jnp.where(mask, lane_gather(tile, lanes), found)
    return found


def running_sum(values, rows, row_ids):
    shift = 1
    while shift < rows:
        moved = pltpu.roll(values, shift, 0)
        values = values + jnp.where(row_ids >= shift, moved, 0.0)
        shift *= 2
    return values


def kernel(
    n_space, n_level, rows, blocks, near_count,
    vel, den, ele, grad, lap, cor, area, thick, send, near, bot,
    vel_out, den_out, ele_out, drift_out,
    own, eta, lanes_of, block_of, east_of, north_of, smooth_of, flow_of,
    held, press, flow, small, out, halo, halo_small, peer,
    vol, vol_all,
    main_send, main_recv, hs_send, hs_recv, peer_send, peer_recv, vol_send, vol_recv,
):
    sp = lax.axis_index("space")
    lv = lax.axis_index("level")
    has = (sp > 0, sp < n_space - 1)
    ends = (sp - 1, sp + 1)

    barrier = pltpu.get_barrier_semaphore()

    def greet(d, _):
        pl.semaphore_signal(barrier, inc=1, device_id={"space": lax.rem(sp + d, n_space), "level": lv})
        return 0

    lax.fori_loop(1, n_space, greet, 0)
    for d in range(1, n_level):
        q = lax.rem(lv + d, n_level)
        pl.semaphore_signal(barrier, inc=1, device_id={"space": sp, "level": q})
        for side in range(2):
            @pl.when(has[side])
            def _():
                pl.semaphore_signal(barrier, inc=1, device_id={"space": ends[side], "level": q})

    row_ids = lax.broadcasted_iota(jnp.int32, (rows, LANES), 0)
    eight = lax.broadcasted_iota(jnp.int32, (8, LANES), 0)
    level_ids = row_ids + lv * rows
    thickness = jnp.zeros((rows, LANES), jnp.float32)
    for r in range(rows):
        thickness = jnp.where(row_ids == r, thick[r], thickness)

    def wide(row, count=rows):
        return jnp.broadcast_to(row, (count, LANES))

    low = jnp.where(has[0], 1, 0)
    high = jnp.where(has[1], 1, 0)

    def prepare(t, _):
        here = pl.ds(pl.multiple_of(t * LANES, LANES), LANES)
        bottom = wide(bot[pl.ds(t, 1), :])
        wet = level_ids < bottom
        own[0, t] = jnp.where(wet, vel[0, :, here], 0.0)
        own[1, t] = jnp.where(wet, vel[1, :, here], 0.0)
        own[2, t] = den[:, here]
        eta[t] = wide(ele[pl.ds(t, 1), :], 8)
        for k in range(near_count):
            slot = wide(near[k:k + 1, here])
            block = lax.shift_right_logical(slot, 7)
            inside = jnp.where(block < blocks, 1, jnp.where(block == blocks, low, high))
            valid = inside > 0
            lanes_of[t, k] = jnp.bitwise_and(slot, LANES - 1)
            block_of[t, k] = jnp.where(valid, block, 0)
            east = jnp.where(valid, wide(grad[0, k:k + 1, here]), 0.0)
            north = jnp.where(valid, wide(grad[1, k:k + 1, here]), 0.0)
            east_of[t, k] = east
            north_of[t, k] = north
            smooth_of[t, k] = jnp.where(valid, wide(lap[k:k + 1, here]), 0.0)
            flow_of[t, k] = jnp.where(eight == 0, east[:8], jnp.where(eight == 1, north[:8], 0.0))
        return 0

    lax.fori_loop(0, blocks, prepare, 0)
    wet_area = area[...] * jnp.where(bot[...] > 0, 1.0, 0.0)
    vol[...] = jnp.where(eight == STEPS, wide(jnp.sum(wet_area, axis=0, keepdims=True), 8), 0.0)

    def main_copy(s, side):
        return pltpu.make_async_remote_copy(
            src_ref=out.at[s, side], dst_ref=halo.at[s, 1 - side],
            send_sem=main_send.at[s, side], recv_sem=main_recv.at[s, 1 - side],
            device_id={"space": ends[side], "level": lv}, device_id_type=pl.DeviceIdType.MESH)

    def small_copy(s, side, q, slot):
        return pltpu.make_async_remote_copy(
            src_ref=out.at[s, side, pl.ds(3 * rows, 8)], dst_ref=halo_small.at[s, 1 - side, slot],
            send_sem=hs_send.at[s, side, q], recv_sem=hs_recv.at[s, 1 - side, slot],
            device_id={"space": ends[side], "level": q}, device_id_type=pl.DeviceIdType.MESH)

    def peer_copy(s, q, slot):
        return pltpu.make_async_remote_copy(
            src_ref=small.at[s], dst_ref=peer.at[s, slot],
            send_sem=peer_send.at[s, q], recv_sem=peer_recv.at[s, slot],
            device_id={"space": sp, "level": q}, device_id_type=pl.DeviceIdType.MESH)

    def vol_copy(q, slot):
        return pltpu.make_async_remote_copy(
            src_ref=vol, dst_ref=vol_all.at[slot],
            send_sem=vol_send.at[q], recv_sem=vol_recv.at[slot],
            device_id={"space": q, "level": lv}, device_id_type=pl.DeviceIdType.MESH)

    others = [lax.rem(lv + d, n_level) for d in range(1, n_level)]

    def make_small(s):
        def body(t, _):
            total = jnp.sum(own[2, t] * thickness, axis=0, keepdims=True)
            flow0 = jnp.sum(own[0, t] * thickness, axis=0, keepdims=True)
            flow1 = jnp.sum(own[1, t] * thickness, axis=0, keepdims=True)
            tile = jnp.where(eight == 0, wide(flow0, 8), jnp.where(eight == 1, wide(flow1, 8), 0.0))
            tile = jnp.where(eight == 2, wide(total, 8), tile)
            small[s, t] = jnp.where(eight == 3, eta[t], tile)
            return 0
        lax.fori_loop(0, blocks, body, 0, unroll=True)

    def send_out(s):
        for side in range(2):
            slot = wide(send[:, side * LANES:(side + 1) * LANES])
            lanes = jnp.bitwise_and(slot, LANES - 1)
            block = lax.shift_right_logical(slot, 7)
            masks = [block == b for b in range(1, blocks)]
            for g in range(3):
                out[s, side, g * rows:(g + 1) * rows] = pick([own[g, b] for b in range(blocks)], lanes, masks)
            out[s, side, 3 * rows:3 * rows + 8] = pick(
                [small[s, b] for b in range(blocks)], lanes[:8], [m[:8] for m in masks])
        for q in others:
            peer_copy(s, q, lv).start()
        for side in range(2):
            @pl.when(has[side])
            def _():
                for q in others:
                    small_copy(s, side, q, lv).start()
                main_copy(s, side).start()

    def gather_own():
        def body(t, _):
            tiles = [[own[g, b] for b in range(blocks)] for g in range(3)]
            for k in range(near_count):
                lanes = lanes_of[t, k]
                block = block_of[t, k]
                masks = [block == b for b in range(1, blocks)]
                for g in range(3):
                    held[t, k, g] = pick(tiles[g], lanes, masks)
            return 0
        lax.fori_loop(0, blocks, body, 0)

    def receive(s):
        for q in others:
            peer_copy(s, q, q).wait_recv()
        for side in range(2):
            @pl.when(has[side])
            def _():
                main_copy(s, 1 - side).wait_recv()
                for q in others:
                    small_copy(s, 1 - side, q, q).wait_recv()

    def close(s):
        for q in others:
            peer_copy(s, q, lv).wait_send()
        for side in range(2):
            @pl.when(has[side])
            def _():
                main_copy(s, side).wait_send()
                for q in others:
                    small_copy(s, side, q, lv).wait_send()

    def columns(s):
        def finish(slot, density, mine, pieces):
            above = jnp.zeros((1, LANES), jnp.float32)
            total = mine
            for q, piece in zip(others, pieces):
                total = total + piece
                above = above + jnp.where(q < lv, piece[2:3], 0.0)
            weighted = density * thickness
            column = wide(above) + running_sum(weighted, rows, row_ids) - 0.5 * weighted
            press[slot] = wide(mine[3:4]) + buoyancy * column
            flow[slot] = total

        def body(t, _):
            finish(t, own[2, t], small[s, t], [peer[s, q, t] for q in others])
            return 0
        lax.fori_loop(0, blocks, body, 0, unroll=True)
        for side in range(2):
            finish(blocks + side, halo[s, side, 2 * rows:3 * rows], halo[s, side, 3 * rows:3 * rows + 8],
                   [halo_small[s, side, q] for q in others])

    def surface(s):
        tiles = [flow[b] for b in range(blocks + 2)]

        def body(t, volume):
            middle = flow[t]
            total = jnp.zeros((8, LANES), jnp.float32)
            for k in range(near_count):
                block = block_of[t, k][:8]
                masks = [block == b for b in range(1, blocks + 2)]
                found = pick(tiles, lanes_of[t, k][:8], masks)
                total = total + flow_of[t, k] * jnp.where(eight < 2, found - middle, 0.0)
            diverge = jnp.sum(total, axis=0, keepdims=True)
            wet_node = jnp.where(bot[pl.ds(t, 1), :] > 0, 1.0, 0.0)
            part = wet_node * diverge
            eta[t] = eta[t] - time_step * wide(part, 8)
            return volume + area[pl.ds(t, 1), :] * part

        volume = lax.fori_loop(0, blocks, body, jnp.zeros((1, LANES), jnp.float32))
        vol[...] = jnp.where(eight == s, wide(volume, 8), vol[...])

    def advance(s):
        pressures = [press[b] for b in range(blocks + 2)]
        edges = [[halo[s, side, g * rows:(g + 1) * rows] for side in range(2)] for g in range(3)]

        def body(t, _):
            here = [own[0, t], own[1, t], own[2, t], press[t]]
            zero = jnp.zeros((rows, LANES), jnp.float32)
            lap0 = lap1 = lap2 = east2 = north2 = east3 = north3 = zero
            for k in range(near_count):
                lanes = lanes_of[t, k]
                block = block_of[t, k]
                masks = [block == b for b in range(1, blocks + 2)]
                diff = []
                for g in range(3):
                    found = held[t, k, g]
                    for side in range(2):
                        found = jnp.where(masks[blocks - 1 + side], lane_gather(edges[g][side], lanes), found)
                    diff.append(found - here[g])
                diff.append(pick(pressures, lanes, masks) - here[3])
                east, north, smooth = east_of[t, k], north_of[t, k], smooth_of[t, k]
                lap0 = lap0 + smooth * diff[0]
                lap1 = lap1 + smooth * diff[1]
                lap2 = lap2 + smooth * diff[2]
                east2 = east2 + east * diff[2]
                north2 = north2 + north * diff[2]
                east3 = east3 + east * diff[3]
                north3 = north3 + north * diff[3]
            bottom = wide(bot[pl.ds(t, 1), :])
            turn = wide(cor[pl.ds(t, 1), :])
            drag = jnp.where(level_ids == bottom - 1, drag_rate, 0.0)
            u, v, rho = here[:3]
            push0 = -east3 + turn * v + lap0 - drag * u
            push1 = -north3 - turn * u + lap1 - drag * v
            wet = level_ids < bottom
            own[0, t] = jnp.where(wet, u + time_step * push0, 0.0)
            own[1, t] = jnp.where(wet, v + time_step * push1, 0.0)
            own[2, t] = rho + time_step * (lap2 - u * east2 - v * north2)
            return 0
        lax.fori_loop(0, blocks, body, 0)

    expected = (n_space - 1) + (n_level - 1) * (1 + low + high)
    pl.semaphore_wait(barrier, expected)

    def step(s, _):
        make_small(s)
        send_out(s)
        gather_own()
        receive(s)
        columns(s)
        surface(s)

        @pl.when(s == STEPS - 1)
        def _():
            def start(d, _):
                vol_copy(lax.rem(sp + d, n_space), sp).start()
                return 0
            lax.fori_loop(1, n_space, start, 0)

        advance(s)
        close(s)
        return 0

    lax.fori_loop(0, STEPS, step, 0)

    for t in range(blocks):
        here = slice(t * LANES, (t + 1) * LANES)
        vel_out[0, :, here] = own[0, t]
        vel_out[1, :, here] = own[1, t]
        den_out[:, here] = own[2, t]

    def collect(d, total):
        q = lax.rem(sp + d, n_space)
        vol_copy(q, q).wait_recv()
        return total + vol_all[q]

    total = lax.fori_loop(1, n_space, collect, vol[...])
    sums = jnp.sum(total, axis=1, keepdims=True)
    drifts = sums / sums[STEPS:STEPS + 1]
    shift = jnp.sum(drifts[:STEPS], axis=0, keepdims=True)
    for t in range(blocks):
        ele_out[t:t + 1, :] = eta[t][:1] + time_step * shift
    drift_out[...] = jnp.broadcast_to(drifts, (8, LANES))

    def finish(d, _):
        vol_copy(lax.rem(sp + d, n_space), sp).wait_send()
        return 0

    lax.fori_loop(1, n_space, finish, 0)


def solution(mesh):
    n_space, n_level = mesh.shape["space"], mesh.shape["level"]

    def local(velocity, density, elevation, grad_weights, lap_weights, coriolis,
              node_area, thickness, send_list, neighbours, bottom):
        rows, nodes = density.shape
        blocks = nodes // LANES
        near_count = neighbours.shape[0]
        f32, i32 = jnp.float32, jnp.int32
        plane = (blocks, LANES)
        vmem = pl.BlockSpec(memory_space=pltpu.VMEM)
        smem = pl.BlockSpec(memory_space=pltpu.SMEM)
        dma = pltpu.SemaphoreType.DMA
        tile = (rows, LANES)
        out = pl.pallas_call(
            functools.partial(kernel, n_space, n_level, rows, blocks, near_count),
            out_shape=(
                jax.ShapeDtypeStruct(velocity.shape, f32),
                jax.ShapeDtypeStruct(density.shape, f32),
                jax.ShapeDtypeStruct(plane, f32),
                jax.ShapeDtypeStruct((8, LANES), f32),
            ),
            in_specs=[vmem] * 7 + [smem] + [vmem] * 3,
            out_specs=(vmem,) * 4,
            scratch_shapes=[
                pltpu.VMEM((3, blocks) + tile, f32),
                pltpu.VMEM((blocks, 8, LANES), f32),
                pltpu.VMEM((blocks, near_count) + tile, i32),
                pltpu.VMEM((blocks, near_count) + tile, i32),
                pltpu.VMEM((blocks, near_count) + tile, f32),
                pltpu.VMEM((blocks, near_count) + tile, f32),
                pltpu.VMEM((blocks, near_count) + tile, f32),
                pltpu.VMEM((blocks, near_count, 8, LANES), f32),
                pltpu.VMEM((blocks, near_count, 3) + tile, f32),
                pltpu.VMEM((blocks + 2,) + tile, f32),
                pltpu.VMEM((blocks + 2, 8, LANES), f32),
                pltpu.VMEM((STEPS, blocks, 8, LANES), f32),
                pltpu.VMEM((STEPS, 2, 3 * rows + 8, LANES), f32),
                pltpu.VMEM((STEPS, 2, 3 * rows + 8, LANES), f32),
                pltpu.VMEM((STEPS, 2, n_level, 8, LANES), f32),
                pltpu.VMEM((STEPS, n_level, blocks, 8, LANES), f32),
                pltpu.VMEM((8, LANES), f32),
                pltpu.VMEM((n_space, 8, LANES), f32),
                dma((STEPS, 2)), dma((STEPS, 2)),
                dma((STEPS, 2, n_level)), dma((STEPS, 2, n_level)),
                dma((STEPS, n_level)), dma((STEPS, n_level)),
                dma((n_space,)), dma((n_space,)),
            ],
            compiler_params=pltpu.CompilerParams(collective_id=0, has_side_effects=True),
        )(velocity, density, elevation.reshape(plane), grad_weights, lap_weights,
          coriolis.reshape(plane), node_area.reshape(plane), thickness, send_list,
          neighbours, bottom.reshape(plane))
        return out[0], out[1], out[2].reshape(nodes), out[3][:STEPS, 0]

    return jax.shard_map(
        local,
        mesh=mesh,
        in_specs=(
            P(None, "level", "space"),
            P("level", "space"),
            P("space"),
            P(None, None, "space"),
            P(None, "space"),
            P("space"),
            P("space"),
            P("level"),
            P("space", None),
            P(None, "space"),
            P("space"),
        ),
        out_specs=(P(None, "level", "space"), P("level", "space"), P("space"), P()),
        check_vma=False,
    )
```

time: 276 us -> 45.1 us (0.16)
  local copies, waits for them, and re-layouts: 127 us -> 5.5 us
  blocking collectives: 60.4 us -> 0 us
  other arithmetic: 45.6 us -> 0 us
  Pallas kernels: 0 us -> 38.7 us
  starting transfers between devices: 24.1 us -> 0 us
  waiting for transfers between devices: 14.7 us -> 0 us
    gather x10 -> x0, local copies, waits for them, and re-layouts: 121 us -> none  [the longest x4 83.6 us: neighbour_terms(): nearby = jnp.take(node_major, neighbours.reshape(-1), axis=0)]
    psum x5 -> x0, blocking collectives: 53.2 us -> none  [the longest x1 40 us: local(): lax.psum((jnp.stack(volume_terms), area_local), 'space')]
    pallas_call x0 -> x1, Pallas kernels: none -> 38.7 us  [local(): pl.pallas_call(functools.partial(kernel, n_space, n_level, rows, blocks,...]
    ppermute x8 -> x0, starting transfers between devices: 24.1 us -> none  [the longest x4 18.9 us: extended_2(): before = lax.ppermute(last, axis, up)]
    select_n x11 -> x0, other arithmetic: 20.2 us -> none  [the longest x4 18.7 us: neighbour_terms(): nearby = jnp.take(node_major, neighbours.reshape(-1), axis=0)]
    ppermute x8 -> x0, waiting for transfers between devices: 14.7 us -> none  [the longest x4 13.1 us: extended_2(): after = lax.ppermute(first, axis, down)]
    unnamed x5 -> x0, other arithmetic: 12.7 us -> none
    all_gather x4 -> x0, blocking collectives: 7.27 us -> none  [prefix(): pieces = lax.all_gather(value, axis)]
  transfers between devices with their start and end apart: 8 -> 0, of which waited for: 6 -> 0; matrix products, arithmetic and copies ran while one was open for 14% -> 0% of each run, Pallas kernels for 0% -> 0%
where the time goes in v1:
time: 45.1 us; the launch traced here: 44.8 us
  Pallas kernels  38.7 us (86%)
  local copies, waits for them, and re-layouts  5.5 us (12%)
  between operations  0.65 us (1%)
    pallas_call x1, Pallas kernels, local(): pl.pallas_call(functools.partial(kernel, n_space, n_level, rows, blocks,...  38.7 us
    unnamed x10, local copies, waits for them, and re-layouts  4.87 us

profile of v1, /device:TPU:0, one launch (start us, length us, event | category | flops | bytes accessed | tf_op | source)
XLA Modules:
  0.0 44.8 jit_solution(12764343661416955862)
XLA Ops:
  0.6 1.4 %copy.16.grad = f32[2,6,1024]{2,1,0:T(8,128)} copy(f32[2,6,1024]{2,0,1:T(2,128)} %param.14) | data formatting | bytes 98304 | tf_op args[3]
  2.1 38.7 %shard_map.138 = (f32[2,8,1024]{2,1,0:T(8,128)}, f32[8,1024]{1,0:T(8,128)}, f32[8,128]{1,0:T(8,128)}, f32[8,128]{1,0:T(8,128)}) custom-call(f32[2,8,1024]{2,1,0:T(8,128)} %vel.1, f32[8,1024]{1,0:T(8,128)} %den.1, f32[8,128]{1,0:T(8,128)} %bitcast.5, f32[2,6,1024]{2,1,0:T(8,128)} %copy.16.grad, f32[6,1024]{1,0:T(8,128)} %lap.1, f32[8,128]{1,0:T(8,128)} %bitcast.6, ...), custom_call_target="tpu_custom_call" | custom-call | tf_op jit(solution)/shard_map/pallas_call | solution.py:339
  40.7 0.0 copy-start.2
  40.8 0.7 %copy-done.2 = f32[8,128]{1,0:T(8,128)S(1)} copy-done((f32[8,128]{1,0:T(8,128)S(1)}, f32[8,128]{1,0:T(8,128)}, u32[]{:S(2)}) %copy-start.2) | copy-done | bytes 4120
  41.4 0.6 %slice_reduce_fusion = f32[4]{0:T(128)} fusion(f32[8,128]{1,0:T(8,128)S(1)} %copy-done.2), kind=kLoop, calls=%fused_computation | loop fusion | bytes 32 | tf_op jit(solution)/shard_map/slice | solution.py:377
  42.1 0.0 copy-start
  42.1 1.5 %copy.20 = f32[2,8,1024]{2,1,0:T(8,128)} copy(f32[2,8,1024]{2,1,0:T(8,128)} %get-tuple-element.16) | data formatting | bytes 131072
  43.5 0.0 copy-done
  43.5 0.0 copy-start.1
  43.5 0.6 %copy.21 = f32[8,1024]{1,0:T(8,128)} copy(f32[8,1024]{1,0:T(8,128)S(1)} %copy-done) | data formatting | bytes 65536
  44.2 0.1 copy-done.1
  44.2 0.6 %copy.22 = f32[1024]{0:T(1024)} copy(f32[1024]{0:T(1024)S(1)} %bitcast.9) | data formatting | bytes 8192
Async XLA Ops:
  40.7 0.7 %copy-start.2 = (f32[8,128]{1,0:T(8,128)S(1)}, f32[8,128]{1,0:T(8,128)}, u32[]{:S(2)}) copy-start(f32[8,128]{1,0:T(8,128)} %get-tuple-element.11) | copy-start | bytes 12292
  42.1 1.5 %copy-start = (f32[8,1024]{1,0:T(8,128)S(1)}, f32[8,1024]{1,0:T(8,128)}, u32[]{:S(2)}) copy-start(f32[8,1024]{1,0:T(8,128)} %get-tuple-element.17) | copy-start | bytes 98308
  43.5 0.7 %copy-start.1 = (f32[8,128]{1,0:T(8,128)S(1)}, f32[8,128]{1,0:T(8,128)}, u32[]{:S(2)}) copy-start(f32[8,128]{1,0:T(8,128)} %get-tuple-element.10) | copy-start | bytes 12292

commit v2 on v1

--- a/solution.py
+++ b/solution.py
@@ -39,8 +39,8 @@
     n_space, n_level, rows, blocks, near_count,
     vel, den, ele, grad, lap, cor, area, thick, send, near, bot,
     vel_out, den_out, ele_out, drift_out,
-    own, eta, lanes_of, block_of, east_of, north_of, smooth_of, flow_of,
-    held, press, flow, small, out, halo, halo_small, peer,
+    own, eta, lanes_of, block_of, east_of, north_of, smooth_of,
+    flow_lanes, flow_block, flow_of, held, flow_held, press, flow, small, out, halo, halo_small, peer,
     vol, vol_all,
     main_send, main_recv, hs_send, hs_recv, peer_send, peer_recv, vol_send, vol_recv,
 ):
@@ -66,6 +66,7 @@
 
     row_ids = lax.broadcasted_iota(jnp.int32, (rows, LANES), 0)
     eight = lax.broadcasted_iota(jnp.int32, (8, LANES), 0)
+    odd = jnp.bitwise_and(eight, 1) == 1
     level_ids = row_ids + lv * rows
     thickness = jnp.zeros((rows, LANES), jnp.float32)
     for r in range(rows):
@@ -92,12 +93,25 @@
             valid = inside > 0
             lanes_of[t, k] = jnp.bitwise_and(slot, LANES - 1)
             block_of[t, k] = jnp.where(valid, block, 0)
-            east = jnp.where(valid, wide(grad[0, k:k + 1, here]), 0.0)
-            north = jnp.where(valid, wide(grad[1, k:k + 1, here]), 0.0)
+            east = jnp.where(valid, wide(grad[k, 0:1, here]), 0.0)
+            north = jnp.where(valid, wide(grad[k, 1:2, here]), 0.0)
             east_of[t, k] = east
             north_of[t, k] = north
             smooth_of[t, k] = jnp.where(valid, wide(lap[k:k + 1, here]), 0.0)
-            flow_of[t, k] = jnp.where(eight == 0, east[:8], jnp.where(eight == 1, north[:8], 0.0))
+        for j in range(flow_of.shape[1]):
+            lane_pack = jnp.zeros((8, LANES), jnp.int32)
+            block_pack = jnp.zeros((8, LANES), jnp.int32)
+            pack = jnp.zeros((8, LANES), jnp.float32)
+            for k in range(4 * j, min(4 * j + 4, near_count)):
+                first = 2 * (k - 4 * j)
+                mine = jnp.logical_or(eight == first, eight == first + 1)
+                lane_pack = jnp.where(mine, lanes_of[t, k, :8], lane_pack)
+                block_pack = jnp.where(mine, block_of[t, k, :8], block_pack)
+                pack = jnp.where(eight == first, east_of[t, k, :8], pack)
+                pack = jnp.where(eight == first + 1, north_of[t, k, :8], pack)
+            flow_lanes[t, j] = lane_pack
+            flow_block[t, j] = block_pack
+            flow_of[t, j] = pack
         return 0
 
     lax.fori_loop(0, blocks, prepare, 0)
@@ -173,8 +187,6 @@
         lax.fori_loop(0, blocks, body, 0)
 
     def receive(s):
-        for q in others:
-            peer_copy(s, q, q).wait_recv()
         for side in range(2):
             @pl.when(has[side])
             def _():
@@ -192,49 +204,65 @@
                 for q in others:
                     small_copy(s, side, q, lv).wait_send()
 
-    def columns(s):
-        def finish(slot, density, mine, pieces):
-            above = jnp.zeros((1, LANES), jnp.float32)
-            total = mine
-            for q, piece in zip(others, pieces):
-                total = total + piece
-                above = above + jnp.where(q < lv, piece[2:3], 0.0)
-            weighted = density * thickness
-            column = wide(above) + running_sum(weighted, rows, row_ids) - 0.5 * weighted
-            press[slot] = wide(mine[3:4]) + buoyancy * column
-            flow[slot] = total
-
+    def finish_column(slot, density, mine, pieces):
+        above = jnp.zeros((1, LANES), jnp.float32)
+        total = mine
+        for q, piece in zip(others, pieces):
+            total = total + piece
+            above = above + jnp.where(q < lv, piece[2:3], 0.0)
+        weighted = density * thickness
+        column = wide(above) + running_sum(weighted, rows, row_ids) - 0.5 * weighted
+        press[slot] = wide(mine[3:4]) + buoyancy * column
+        flow[slot] = jnp.where(odd, wide(total[1:2], 8), wide(total[0:1], 8))
+
+    def own_columns(s):
         def body(t, _):
-            finish(t, own[2, t], small[s, t], [peer[s, q, t] for q in others])
+            finish_column(t, own[2, t], small[s, t], [peer[s, q, t] for q in others])
             return 0
         lax.fori_loop(0, blocks, body, 0, unroll=True)
-        for side in range(2):
-            finish(blocks + side, halo[s, side, 2 * rows:3 * rows], halo[s, side, 3 * rows:3 * rows + 8],
-                   [halo_small[s, side, q] for q in others])
+
+    def halo_columns(s):
+        for side in range(2):
+            finish_column(blocks + side, halo[s, side, 2 * rows:3 * rows], halo[s, side, 3 * rows:3 * rows + 8],
+                          [halo_small[s, side, q] for q in others])
+
+    def gather_columns():
+        pressures = [press[b] for b in range(blocks)]
+        flows = [flow[b] for b in range(blocks)]
+
+        def body(t, _):
+            for k in range(near_count):
+                block = block_of[t, k]
+                held[t, k, 3] = pick(pressures, lanes_of[t, k], [block == b for b in range(1, blocks)])
+            for j in range(flow_of.shape[1]):
+                block = flow_block[t, j]
+                flow_held[t, j] = pick(flows, flow_lanes[t, j], [block == b for b in range(1, blocks)])
+            return 0
+        lax.fori_loop(0, blocks, body, 0)
 
     def surface(s):
-        tiles = [flow[b] for b in range(blocks + 2)]
+        sides = [flow[blocks], flow[blocks + 1]]
 
         def body(t, volume):
             middle = flow[t]
             total = jnp.zeros((8, LANES), jnp.float32)
-            for k in range(near_count):
-                block = block_of[t, k][:8]
-                masks = [block == b for b in range(1, blocks + 2)]
-                found = pick(tiles, lanes_of[t, k][:8], masks)
-                total = total + flow_of[t, k] * jnp.where(eight < 2, found - middle, 0.0)
+            for j in range(flow_of.shape[1]):
+                lanes, block, found = flow_lanes[t, j], flow_block[t, j], flow_held[t, j]
+                for side in range(2):
+                    found = jnp.where(block == blocks + side, lane_gather(sides[side], lanes), found)
+                total = total + flow_of[t, j] * (found - middle)
             diverge = jnp.sum(total, axis=0, keepdims=True)
             wet_node = jnp.where(bot[pl.ds(t, 1), :] > 0, 1.0, 0.0)
             part = wet_node * diverge
             eta[t] = eta[t] - time_step * wide(part, 8)
             return volume + area[pl.ds(t, 1), :] * part
 
-        volume = lax.fori_loop(0, blocks, body, jnp.zeros((1, LANES), jnp.float32))
+        volume = lax.fori_loop(0, blocks, body, jnp.zeros((1, LANES), jnp.float32), unroll=True)
         vol[...] = jnp.where(eight == s, wide(volume, 8), vol[...])
 
     def advance(s):
-        pressures = [press[b] for b in range(blocks + 2)]
         edges = [[halo[s, side, g * rows:(g + 1) * rows] for side in range(2)] for g in range(3)]
+        edges.append([press[blocks], press[blocks + 1]])
 
         def body(t, _):
             here = [own[0, t], own[1, t], own[2, t], press[t]]
@@ -243,14 +271,13 @@
             for k in range(near_count):
                 lanes = lanes_of[t, k]
                 block = block_of[t, k]
-                masks = [block == b for b in range(1, blocks + 2)]
+                masks = [block == blocks, block == blocks + 1]
                 diff = []
-                for g in range(3):
+                for g in range(4):
                     found = held[t, k, g]
                     for side in range(2):
-                        found = jnp.where(masks[blocks - 1 + side], lane_gather(edges[g][side], lanes), found)
+                        found = jnp.where(masks[side], lane_gather(edges[g][side], lanes), found)
                     diff.append(found - here[g])
-                diff.append(pick(pressures, lanes, masks) - here[3])
                 east, north, smooth = east_of[t, k], north_of[t, k], smooth_of[t, k]
                 lap0 = lap0 + smooth * diff[0]
                 lap1 = lap1 + smooth * diff[1]
@@ -279,8 +306,12 @@
         make_small(s)
         send_out(s)
         gather_own()
+        for q in others:
+            peer_copy(s, q, q).wait_recv()
+        own_columns(s)
+        gather_columns()
         receive(s)
-        columns(s)
+        halo_columns(s)
         surface(s)
 
         @pl.when(s == STEPS - 1)
@@ -330,6 +361,7 @@
         rows, nodes = density.shape
         blocks = nodes // LANES
         near_count = neighbours.shape[0]
+        packs = -(-near_count // 4)
         f32, i32 = jnp.float32, jnp.int32
         plane = (blocks, LANES)
         vmem = pl.BlockSpec(memory_space=pltpu.VMEM)
@@ -354,8 +386,11 @@
                 pltpu.VMEM((blocks, near_count) + tile, f32),
                 pltpu.VMEM((blocks, near_count) + tile, f32),
                 pltpu.VMEM((blocks, near_count) + tile, f32),
-                pltpu.VMEM((blocks, near_count, 8, LANES), f32),
-                pltpu.VMEM((blocks, near_count, 3) + tile, f32),
+                pltpu.VMEM((blocks, packs, 8, LANES), i32),
+                pltpu.VMEM((blocks, packs, 8, LANES), i32),
+                pltpu.VMEM((blocks, packs, 8, LANES), f32),
+                pltpu.VMEM((blocks, near_count, 4) + tile, f32),
+                pltpu.VMEM((blocks, packs, 8, LANES), f32),
                 pltpu.VMEM((blocks + 2,) + tile, f32),
                 pltpu.VMEM((blocks + 2, 8, LANES), f32),
                 pltpu.VMEM((STEPS, blocks, 8, LANES), f32),
@@ -371,7 +406,7 @@
                 dma((n_space,)), dma((n_space,)),
             ],
             compiler_params=pltpu.CompilerParams(collective_id=0, has_side_effects=True),
-        )(velocity, density, elevation.reshape(plane), grad_weights, lap_weights,
+        )(velocity, density, elevation.reshape(plane), grad_weights.transpose(1, 0, 2), lap_weights,
           coriolis.reshape(plane), node_area.reshape(plane), thickness, send_list,
           neighbours, bottom.reshape(plane))
         return out[0], out[1], out[2].reshape(nodes), out[3][:STEPS, 0]

time: 45.1 us -> 36.9 us (0.82)
  Pallas kernels: 38.7 us -> 31.9 us
  local copies, waits for them, and re-layouts: 5.5 us -> 4.05 us
    pallas_call x1, Pallas kernels: 38.7 us -> 31.9 us  [local(): pl.pallas_call(functools.partial(kernel, n_space, n_level, rows, blocks,...]
    unnamed x10 -> x9, local copies, waits for them, and re-layouts: 4.87 us -> 3.43 us
where the time goes in v2:
time: 36.9 us; the launch traced here: 36.6 us
  Pallas kernels  31.9 us (86%)
  local copies, waits for them, and re-layouts  4.05 us (11%)
  between operations  0.66 us (2%)
    pallas_call x1, Pallas kernels, local(): pl.pallas_call(functools.partial(kernel, n_space, n_level, rows, blocks,...  31.9 us
    unnamed x9, local copies, waits for them, and re-layouts  3.43 us

profile of v2, /device:TPU:0, one launch (start us, length us, event | category | flops | bytes accessed | tf_op | source)
XLA Modules:
  0.0 36.6 jit_solution(7626472763149720233)
XLA Ops:
  0.6 31.9 %shard_map.138 = (f32[2,8,1024]{2,1,0:T(8,128)}, f32[8,1024]{1,0:T(8,128)}, f32[8,128]{1,0:T(8,128)}, f32[8,128]{1,0:T(8,128)}) custom-call(f32[2,8,1024]{2,1,0:T(8,128)} %vel.1, f32[8,1024]{1,0:T(8,128)} %den.1, f32[8,128]{1,0:T(8,128)} %bitcast.7, f32[6,2,1024]{2,1,0:T(2,128)} %bitcast.6, f32[6,1024]{1,0:T(8,128)} %lap.1, f32[8,128]{1,0:T(8,128)} %bitcast.8, ...), custom_call_target="tpu_custom_call" | custom-call | tf_op jit(solution)/shard_map/pallas_call | solution.py:371
  32.5 0.0 copy-start.2
  32.5 0.7 %copy-done.2 = f32[8,128]{1,0:T(8,128)S(1)} copy-done((f32[8,128]{1,0:T(8,128)S(1)}, f32[8,128]{1,0:T(8,128)}, u32[]{:S(2)}) %copy-start.2) | copy-done | bytes 4120
  33.2 0.6 %slice_reduce_fusion = f32[4]{0:T(128)} fusion(f32[8,128]{1,0:T(8,128)S(1)} %copy-done.2), kind=kLoop, calls=%fused_computation | loop fusion | bytes 32 | tf_op jit(solution)/shard_map/slice | solution.py:412
  33.8 0.0 copy-start
  33.9 1.5 %copy.18 = f32[2,8,1024]{2,1,0:T(8,128)} copy(f32[2,8,1024]{2,1,0:T(8,128)} %get-tuple-element.16) | data formatting | bytes 131072
  35.3 0.0 copy-done
  35.3 0.0 copy-start.1
  35.3 0.6 %copy.19 = f32[8,1024]{1,0:T(8,128)} copy(f32[8,1024]{1,0:T(8,128)S(1)} %copy-done) | data formatting | bytes 65536
  36.0 0.1 copy-done.1
  36.0 0.6 %copy.20 = f32[1024]{0:T(1024)} copy(f32[1024]{0:T(1024)S(1)} %bitcast.11) | data formatting | bytes 8192
Async XLA Ops:
  32.5 0.7 %copy-start.2 = (f32[8,128]{1,0:T(8,128)S(1)}, f32[8,128]{1,0:T(8,128)}, u32[]{:S(2)}) copy-start(f32[8,128]{1,0:T(8,128)} %get-tuple-element.11) | copy-start | bytes 12292
  33.8 1.5 %copy-start = (f32[8,1024]{1,0:T(8,128)S(1)}, f32[8,1024]{1,0:T(8,128)}, u32[]{:S(2)}) copy-start(f32[8,1024]{1,0:T(8,128)} %get-tuple-element.17) | copy-start | bytes 98308
  35.3 0.7 %copy-start.1 = (f32[8,128]{1,0:T(8,128)S(1)}, f32[8,128]{1,0:T(8,128)}, u32[]{:S(2)}) copy-start(f32[8,128]{1,0:T(8,128)} %get-tuple-element.10) | copy-start | bytes 12292

commit v3 on v2

--- a/solution.py
+++ b/solution.py
@@ -36,13 +36,13 @@
 
 
 def kernel(
-    n_space, n_level, rows, blocks, near_count,
+    n_space, n_level, width, rows, blocks, near_count,
     vel, den, ele, grad, lap, cor, area, thick, send, near, bot,
     vel_out, den_out, ele_out, drift_out,
     own, eta, lanes_of, block_of, east_of, north_of, smooth_of,
     flow_lanes, flow_block, flow_of, held, flow_held, press, flow, small, out, halo, halo_small, peer,
     vol, vol_all,
-    main_send, main_recv, hs_send, hs_recv, peer_send, peer_recv, vol_send, vol_recv,
+    main_send, main_recv, hs_send, hs_recv, peer_send, peer_recv, vol_send, vol_recv, column_in,
 ):
     sp = lax.axis_index("space")
     lv = lax.axis_index("level")
@@ -51,11 +51,15 @@
 
     barrier = pltpu.get_barrier_semaphore()
 
-    def greet(d, _):
-        pl.semaphore_signal(barrier, inc=1, device_id={"space": lax.rem(sp + d, n_space), "level": lv})
-        return 0
-
-    lax.fori_loop(1, n_space, greet, 0)
+    mine, place = sp // width, lax.rem(sp, width)
+    column = [lax.rem(sp + d * width, n_space) for d in range(1, n_space // width)]
+    row = [mine * width + lax.rem(place + d, width) for d in range(1, width)]
+    for q in row + column:
+        pl.semaphore_signal(barrier, inc=1, device_id={"space": q, "level": lv})
+    for side in range(2):
+        @pl.when(has[side])
+        def _():
+            pl.semaphore_signal(barrier, inc=1, device_id={"space": ends[side], "level": lv})
     for d in range(1, n_level):
         q = lax.rem(lv + d, n_level)
         pl.semaphore_signal(barrier, inc=1, device_id={"space": sp, "level": q})
@@ -299,8 +303,10 @@
             return 0
         lax.fori_loop(0, blocks, body, 0)
 
-    expected = (n_space - 1) + (n_level - 1) * (1 + low + high)
+    expected = len(row) + len(column) + low + high + (n_level - 1) * (1 + low + high)
     pl.semaphore_wait(barrier, expected)
+    for q in row:
+        pl.semaphore_signal(column_in, inc=1, device_id={"space": q, "level": lv})
 
     def step(s, _):
         make_small(s)
@@ -316,6 +322,8 @@
 
         @pl.when(s == STEPS - 1)
         def _():
+            pl.semaphore_wait(column_in, len(row))
+
             def start(d, _):
                 vol_copy(lax.rem(sp + d, n_space), sp).start()
                 return 0
@@ -344,7 +352,11 @@
     shift = jnp.sum(drifts[:STEPS], axis=0, keepdims=True)
     for t in range(blocks):
         ele_out[t:t + 1, :] = eta[t][:1] + time_step * shift
-    drift_out[...] = jnp.broadcast_to(drifts, (8, LANES))
+    lane_ids = lax.broadcasted_iota(jnp.int32, (1, LANES), 1)
+    line = jnp.zeros((1, LANES), jnp.float32)
+    for s in range(STEPS):
+        line = jnp.where(lane_ids == s, drifts[s:s + 1], line)
+    drift_out[...] = line
 
     def finish(d, _):
         vol_copy(lax.rem(sp + d, n_space), sp).wait_send()
@@ -353,8 +365,16 @@
     lax.fori_loop(1, n_space, finish, 0)
 
 
+def emit(vel, den, ele, drift, vel_out, den_out, ele_out, drift_out):
+    vel_out[...] = vel[...]
+    den_out[...] = den[...]
+    ele_out[...] = ele[...]
+    drift_out[...] = drift[:, :STEPS]
+
+
 def solution(mesh):
     n_space, n_level = mesh.shape["space"], mesh.shape["level"]
+    width = max(w for w in range(1, n_space + 1) if n_space % w == 0 and w * w <= n_space)
 
     def local(velocity, density, elevation, grad_weights, lap_weights, coriolis,
               node_area, thickness, send_list, neighbours, bottom):
@@ -369,12 +389,12 @@
         dma = pltpu.SemaphoreType.DMA
         tile = (rows, LANES)
         out = pl.pallas_call(
-            functools.partial(kernel, n_space, n_level, rows, blocks, near_count),
+            functools.partial(kernel, n_space, n_level, width, rows, blocks, near_count),
             out_shape=(
                 jax.ShapeDtypeStruct(velocity.shape, f32),
                 jax.ShapeDtypeStruct(density.shape, f32),
                 jax.ShapeDtypeStruct(plane, f32),
-                jax.ShapeDtypeStruct((8, LANES), f32),
+                jax.ShapeDtypeStruct((1, LANES), f32),
             ),
             in_specs=[vmem] * 7 + [smem] + [vmem] * 3,
             out_specs=(vmem,) * 4,
@@ -404,12 +424,24 @@
                 dma((STEPS, 2, n_level)), dma((STEPS, 2, n_level)),
                 dma((STEPS, n_level)), dma((STEPS, n_level)),
                 dma((n_space,)), dma((n_space,)),
+                pltpu.SemaphoreType.REGULAR,
             ],
             compiler_params=pltpu.CompilerParams(collective_id=0, has_side_effects=True),
         )(velocity, density, elevation.reshape(plane), grad_weights.transpose(1, 0, 2), lap_weights,
           coriolis.reshape(plane), node_area.reshape(plane), thickness, send_list,
           neighbours, bottom.reshape(plane))
-        return out[0], out[1], out[2].reshape(nodes), out[3][:STEPS, 0]
+        out = pl.pallas_call(
+            emit,
+            out_shape=(
+                jax.ShapeDtypeStruct(velocity.shape, f32),
+                jax.ShapeDtypeStruct(density.shape, f32),
+                jax.ShapeDtypeStruct(plane, f32),
+                jax.ShapeDtypeStruct((1, STEPS), f32),
+            ),
+            in_specs=[vmem] * 4,
+            out_specs=(vmem,) * 4,
+        )(*out)
+        return out[0], out[1], out[2].reshape(nodes), out[3].reshape(STEPS)
 
     return jax.shard_map(
         local,

time: 36.9 us -> 34.3 us (0.930)
  local copies, waits for them, and re-layouts: 4.05 us -> 0 us
  Pallas kernels: 31.9 us -> 33.4 us
    unnamed x9 -> x0, local copies, waits for them, and re-layouts: 3.43 us -> none
    pallas_call x1 -> x2, Pallas kernels: 31.9 us -> 33.4 us  [the longest x1 31.9 us: local(): pl.pallas_call(functools.partial(kernel, n_space, n_level, width, rows, b...]
    slice x1 -> x0, local copies, waits for them, and re-layouts: 0.63 us -> none  [local(): return (out[0], out[1], out[2].reshape(nodes), out[3][:STEPS, 0])]
where the time goes in v3:
time: 34.3 us; the launch traced here: 34.1 us
  Pallas kernels  33.4 us (97%)
  between operations  0.64 us (2%)
    pallas_call x1, Pallas kernels, local(): pl.pallas_call(functools.partial(kernel, n_space, n_level, width, rows, b...  31.9 us
    pallas_call x1, Pallas kernels, local(): pl.pallas_call(emit, out_shape=(jax.ShapeDtypeStruct(velocity.shape, f32)...  1.51 us

profile of v3, /device:TPU:0, one launch (start us, length us, event | category | flops | bytes accessed | tf_op | source)
XLA Modules:
  0.0 34.1 jit_solution(17550215623060622684)
XLA Ops:
  0.6 31.9 %shard_map.138 = (f32[2,8,1024]{2,1,0:T(8,128)}, f32[8,1024]{1,0:T(8,128)}, f32[8,128]{1,0:T(8,128)}, f32[1,128]{1,0:T(1,128)}) custom-call(f32[2,8,1024]{2,1,0:T(8,128)} %vel.1, f32[8,1024]{1,0:T(8,128)} %den.1, f32[8,128]{1,0:T(8,128)} %bitcast.8, f32[6,2,1024]{2,1,0:T(2,128)} %bitcast.7, f32[6,1024]{1,0:T(8,128)} %lap.1, f32[8,128]{1,0:T(8,128)} %bitcast.9, ...), custom_call_target="tpu_custom_call" | custom-call | tf_op jit(solution)/shard_map/pallas_call | solution.py:391
  32.6 1.5 %shard_map.139 = (f32[2,8,1024]{2,1,0:T(8,128)}, f32[8,1024]{1,0:T(8,128)}, f32[8,128]{1,0:T(8,128)}, f32[1,4]{1,0:T(1,128)}) custom-call(f32[2,8,1024]{2,1,0:T(8,128)} %get-tuple-element.12.vel, f32[8,1024]{1,0:T(8,128)} %get-tuple-element.13.den, f32[8,128]{1,0:T(8,128)} %get-tuple-element.14.ele, f32[1,128]{1,0:T(1,128)} %get-tuple-element.15.drift), custom_call_target="tpu_custom_call" | custom-call | tf_op jit(solution)/shard_map/pallas_call | solution.py:433

commit v4 on v3

--- a/solution.py
+++ b/solution.py
@@ -41,7 +41,7 @@
     vel_out, den_out, ele_out, drift_out,
     own, eta, lanes_of, block_of, east_of, north_of, smooth_of,
     flow_lanes, flow_block, flow_of, held, flow_held, press, flow, small, out, halo, halo_small, peer,
-    vol, vol_all,
+    vol, vol_line, vol_all,
     main_send, main_recv, hs_send, hs_recv, peer_send, peer_recv, vol_send, vol_recv, column_in,
 ):
     sp = lax.axis_index("space")
@@ -71,6 +71,7 @@
     row_ids = lax.broadcasted_iota(jnp.int32, (rows, LANES), 0)
     eight = lax.broadcasted_iota(jnp.int32, (8, LANES), 0)
     odd = jnp.bitwise_and(eight, 1) == 1
+    lane_ids = lax.broadcasted_iota(jnp.int32, (1, LANES), 1)
     level_ids = row_ids + lv * rows
     thickness = jnp.zeros((rows, LANES), jnp.float32)
     for r in range(rows):
@@ -124,7 +125,7 @@
 
     def main_copy(s, side):
         return pltpu.make_async_remote_copy(
-            src_ref=out.at[s, side], dst_ref=halo.at[s, 1 - side],
+            src_ref=out.at[s, side, pl.ds(0, 3 * rows)], dst_ref=halo.at[s, 1 - side],
             send_sem=main_send.at[s, side], recv_sem=main_recv.at[s, 1 - side],
             device_id={"space": ends[side], "level": lv}, device_id_type=pl.DeviceIdType.MESH)
 
@@ -142,7 +143,7 @@
 
     def vol_copy(q, slot):
         return pltpu.make_async_remote_copy(
-            src_ref=vol, dst_ref=vol_all.at[slot],
+            src_ref=vol_line, dst_ref=vol_all.at[slot],
             send_sem=vol_send.at[q], recv_sem=vol_recv.at[slot],
             device_id={"space": q, "level": lv}, device_id_type=pl.DeviceIdType.MESH)
 
@@ -159,7 +160,7 @@
             return 0
         lax.fori_loop(0, blocks, body, 0, unroll=True)
 
-    def send_out(s):
+    def stage_out(s):
         for side in range(2):
             slot = wide(send[:, side * LANES:(side + 1) * LANES])
             lanes = jnp.bitwise_and(slot, LANES - 1)
@@ -169,12 +170,14 @@
                 out[s, side, g * rows:(g + 1) * rows] = pick([own[g, b] for b in range(blocks)], lanes, masks)
             out[s, side, 3 * rows:3 * rows + 8] = pick(
                 [small[s, b] for b in range(blocks)], lanes[:8], [m[:8] for m in masks])
+
+    def send_out(s):
         for q in others:
             peer_copy(s, q, lv).start()
         for side in range(2):
             @pl.when(has[side])
             def _():
-                for q in others:
+                for q in others + [lv]:
                     small_copy(s, side, q, lv).start()
                 main_copy(s, side).start()
 
@@ -190,13 +193,18 @@
             return 0
         lax.fori_loop(0, blocks, body, 0)
 
-    def receive(s):
+    def receive_small(s):
+        for side in range(2):
+            @pl.when(has[side])
+            def _():
+                for q in others + [lv]:
+                    small_copy(s, 1 - side, q, q).wait_recv()
+
+    def receive_main(s):
         for side in range(2):
             @pl.when(has[side])
             def _():
                 main_copy(s, 1 - side).wait_recv()
-                for q in others:
-                    small_copy(s, 1 - side, q, q).wait_recv()
 
     def close(s):
         for q in others:
@@ -205,30 +213,39 @@
             @pl.when(has[side])
             def _():
                 main_copy(s, side).wait_send()
-                for q in others:
+                for q in others + [lv]:
                     small_copy(s, side, q, lv).wait_send()
 
-    def finish_column(slot, density, mine, pieces):
+    def finish_flow(slot, mine, pieces):
+        total = mine
+        for piece in pieces:
+            total = total + piece
+        flow[slot] = jnp.where(odd, wide(total[1:2], 8), wide(total[0:1], 8))
+
+    def finish_press(slot, density, mine, pieces):
         above = jnp.zeros((1, LANES), jnp.float32)
-        total = mine
         for q, piece in zip(others, pieces):
-            total = total + piece
             above = above + jnp.where(q < lv, piece[2:3], 0.0)
         weighted = density * thickness
         column = wide(above) + running_sum(weighted, rows, row_ids) - 0.5 * weighted
         press[slot] = wide(mine[3:4]) + buoyancy * column
-        flow[slot] = jnp.where(odd, wide(total[1:2], 8), wide(total[0:1], 8))
 
     def own_columns(s):
         def body(t, _):
-            finish_column(t, own[2, t], small[s, t], [peer[s, q, t] for q in others])
+            pieces = [peer[s, q, t] for q in others]
+            finish_flow(t, small[s, t], pieces)
+            finish_press(t, own[2, t], small[s, t], pieces)
             return 0
         lax.fori_loop(0, blocks, body, 0, unroll=True)
 
+    def halo_flows(s):
+        for side in range(2):
+            finish_flow(blocks + side, halo_small[s, side, lv], [halo_small[s, side, q] for q in others])
+
     def halo_columns(s):
         for side in range(2):
-            finish_column(blocks + side, halo[s, side, 2 * rows:3 * rows], halo[s, side, 3 * rows:3 * rows + 8],
-                          [halo_small[s, side, q] for q in others])
+            finish_press(blocks + side, halo[s, side, 2 * rows:3 * rows], halo_small[s, side, lv],
+                         [halo_small[s, side, q] for q in others])
 
     def gather_columns():
         pressures = [press[b] for b in range(blocks)]
@@ -301,7 +318,10 @@
             own[1, t] = jnp.where(wet, v + time_step * push1, 0.0)
             own[2, t] = rho + time_step * (lap2 - u * east2 - v * north2)
             return 0
-        lax.fori_loop(0, blocks, body, 0)
+        lax.fori_loop(0, blocks, body, 0, unroll=True)
+
+    make_small(0)
+    stage_out(0)
 
     expected = len(row) + len(column) + low + high + (n_level - 1) * (1 + low + high)
     pl.semaphore_wait(barrier, expected)
@@ -309,19 +329,23 @@
         pl.semaphore_signal(column_in, inc=1, device_id={"space": q, "level": lv})
 
     def step(s, _):
-        make_small(s)
         send_out(s)
         gather_own()
         for q in others:
             peer_copy(s, q, q).wait_recv()
         own_columns(s)
         gather_columns()
-        receive(s)
-        halo_columns(s)
+        receive_small(s)
+        halo_flows(s)
         surface(s)
 
         @pl.when(s == STEPS - 1)
         def _():
+            sums = jnp.sum(vol[...], axis=1, keepdims=True)
+            line = jnp.zeros((1, LANES), jnp.float32)
+            for i in range(STEPS + 1):
+                line = jnp.where(lane_ids == i, sums[i:i + 1], line)
+            vol_line[...] = line
             pl.semaphore_wait(column_in, len(row))
 
             def start(d, _):
@@ -329,7 +353,15 @@
                 return 0
             lax.fori_loop(1, n_space, start, 0)
 
+        receive_main(s)
+        halo_columns(s)
         advance(s)
+
+        @pl.when(s < STEPS - 1)
+        def _():
+            make_small(s + 1)
+            stage_out(s + 1)
+
         close(s)
         return 0
 
@@ -346,17 +378,12 @@
         vol_copy(q, q).wait_recv()
         return total + vol_all[q]
 
-    total = lax.fori_loop(1, n_space, collect, vol[...])
-    sums = jnp.sum(total, axis=1, keepdims=True)
-    drifts = sums / sums[STEPS:STEPS + 1]
-    shift = jnp.sum(drifts[:STEPS], axis=0, keepdims=True)
+    total = lax.fori_loop(1, n_space, collect, vol_line[...])
+    drifts = total / total[:, STEPS:STEPS + 1]
+    shift = jnp.sum(jnp.where(lane_ids < STEPS, drifts, 0.0), axis=1, keepdims=True)
     for t in range(blocks):
         ele_out[t:t + 1, :] = eta[t][:1] + time_step * shift
-    lane_ids = lax.broadcasted_iota(jnp.int32, (1, LANES), 1)
-    line = jnp.zeros((1, LANES), jnp.float32)
-    for s in range(STEPS):
-        line = jnp.where(lane_ids == s, drifts[s:s + 1], line)
-    drift_out[...] = line
+    drift_out[...] = drifts
 
     def finish(d, _):
         vol_copy(lax.rem(sp + d, n_space), sp).wait_send()
@@ -415,11 +442,12 @@
                 pltpu.VMEM((blocks + 2, 8, LANES), f32),
                 pltpu.VMEM((STEPS, blocks, 8, LANES), f32),
                 pltpu.VMEM((STEPS, 2, 3 * rows + 8, LANES), f32),
-                pltpu.VMEM((STEPS, 2, 3 * rows + 8, LANES), f32),
+                pltpu.VMEM((STEPS, 2, 3 * rows, LANES), f32),
                 pltpu.VMEM((STEPS, 2, n_level, 8, LANES), f32),
                 pltpu.VMEM((STEPS, n_level, blocks, 8, LANES), f32),
                 pltpu.VMEM((8, LANES), f32),
-                pltpu.VMEM((n_space, 8, LANES), f32),
+                pltpu.VMEM((1, LANES), f32),
+                pltpu.VMEM((n_space, 1, LANES), f32),
                 dma((STEPS, 2)), dma((STEPS, 2)),
                 dma((STEPS, 2, n_level)), dma((STEPS, 2, n_level)),
                 dma((STEPS, n_level)), dma((STEPS, n_level)),

time: 34.3 us -> 31.7 us (0.924)
  Pallas kernels: 33.4 us -> 30.9 us
    pallas_call x1, Pallas kernels: 31.9 us -> 29.4 us  [local(): pl.pallas_call(functools.partial(kernel, n_space, n_level, width, rows, b...]
where the time goes in v4:
time: 31.7 us; the launch traced here: 31.5 us
  Pallas kernels  30.9 us (97%)
  between operations  0.64 us (2%)
    pallas_call x1, Pallas kernels, local(): pl.pallas_call(functools.partial(kernel, n_space, n_level, width, rows, b...  29.4 us
    pallas_call x1, Pallas kernels, local(): pl.pallas_call(emit, out_shape=(jax.ShapeDtypeStruct(velocity.shape, f32)...  1.51 us

profile of v4, /device:TPU:0, one launch (start us, length us, event | category | flops | bytes accessed | tf_op | source)
XLA Modules:
  0.0 31.5 jit_solution(10627426922953672755)
XLA Ops:
  0.6 29.4 %shard_map.138 = (f32[2,8,1024]{2,1,0:T(8,128)}, f32[8,1024]{1,0:T(8,128)}, f32[8,128]{1,0:T(8,128)}, f32[1,128]{1,0:T(1,128)}) custom-call(f32[2,8,1024]{2,1,0:T(8,128)} %vel.1, f32[8,1024]{1,0:T(8,128)} %den.1, f32[8,128]{1,0:T(8,128)} %bitcast.8, f32[6,2,1024]{2,1,0:T(2,128)} %bitcast.7, f32[6,1024]{1,0:T(8,128)} %lap.1, f32[8,128]{1,0:T(8,128)} %bitcast.9, ...), custom_call_target="tpu_custom_call" | custom-call | tf_op jit(solution)/shard_map/pallas_call | solution.py:418
  30.0 1.5 %shard_map.139 = (f32[2,8,1024]{2,1,0:T(8,128)}, f32[8,1024]{1,0:T(8,128)}, f32[8,128]{1,0:T(8,128)}, f32[1,4]{1,0:T(1,128)}) custom-call(f32[2,8,1024]{2,1,0:T(8,128)} %get-tuple-element.12.vel, f32[8,1024]{1,0:T(8,128)} %get-tuple-element.13.den, f32[8,128]{1,0:T(8,128)} %get-tuple-element.14.ele, f32[1,128]{1,0:T(1,128)} %get-tuple-element.15.drift), custom_call_target="tpu_custom_call" | custom-call | tf_op jit(solution)/shard_map/pallas_call | solution.py:461

commit v5 on v4

--- a/solution.py
+++ b/solution.py
@@ -42,7 +42,7 @@
     own, eta, lanes_of, block_of, east_of, north_of, smooth_of,
     flow_lanes, flow_block, flow_of, held, flow_held, press, flow, small, out, halo, halo_small, peer,
     vol, vol_line, vol_all,
-    main_send, main_recv, hs_send, hs_recv, peer_send, peer_recv, vol_send, vol_recv, column_in,
+    main_send, main_recv, hs_send, hs_recv, peer_send, peer_recv, vol_send, vol_recv, column_in, load_sem, *loaded,
 ):
     sp = lax.axis_index("space")
     lv = lax.axis_index("level")
@@ -67,6 +67,16 @@
             @pl.when(has[side])
             def _():
                 pl.semaphore_signal(barrier, inc=1, device_id={"space": ends[side], "level": q})
+
+    loads = [
+        pltpu.make_async_copy(ref, buffer, load_sem.at[i])
+        for i, (ref, buffer) in enumerate(zip((vel, den, ele, grad, lap, cor, area, send, near, bot), loaded))
+    ]
+    for load in loads:
+        load.start()
+    for load in loads:
+        load.wait()
+    vel, den, ele, grad, lap, cor, area, send, near, bot = loaded
 
     row_ids = lax.broadcasted_iota(jnp.int32, (rows, LANES), 0)
     eight = lax.broadcasted_iota(jnp.int32, (8, LANES), 0)
@@ -412,9 +422,13 @@
         f32, i32 = jnp.float32, jnp.int32
         plane = (blocks, LANES)
         vmem = pl.BlockSpec(memory_space=pltpu.VMEM)
+        hbm = pl.BlockSpec(memory_space=pl.ANY)
         smem = pl.BlockSpec(memory_space=pltpu.SMEM)
         dma = pltpu.SemaphoreType.DMA
         tile = (rows, LANES)
+        arrays = [velocity, density, elevation.reshape(plane), grad_weights.transpose(1, 0, 2), lap_weights,
+                  coriolis.reshape(plane), node_area.reshape(plane), thickness, send_list,
+                  neighbours, bottom.reshape(plane)]
         out = pl.pallas_call(
             functools.partial(kernel, n_space, n_level, width, rows, blocks, near_count),
             out_shape=(
@@ -423,7 +437,7 @@
                 jax.ShapeDtypeStruct(plane, f32),
                 jax.ShapeDtypeStruct((1, LANES), f32),
             ),
-            in_specs=[vmem] * 7 + [smem] + [vmem] * 3,
+            in_specs=[hbm] * 7 + [smem] + [hbm] * 3,
             out_specs=(vmem,) * 4,
             scratch_shapes=[
                 pltpu.VMEM((3, blocks) + tile, f32),
@@ -453,11 +467,10 @@
                 dma((STEPS, n_level)), dma((STEPS, n_level)),
                 dma((n_space,)), dma((n_space,)),
                 pltpu.SemaphoreType.REGULAR,
-            ],
+                dma((10,)),
+            ] + [pltpu.VMEM(a.shape, a.dtype) for a in arrays[:7] + arrays[8:]],
             compiler_params=pltpu.CompilerParams(collective_id=0, has_side_effects=True),
-        )(velocity, density, elevation.reshape(plane), grad_weights.transpose(1, 0, 2), lap_weights,
-          coriolis.reshape(plane), node_area.reshape(plane), thickness, send_list,
-          neighbours, bottom.reshape(plane))
+        )(*arrays)
         out = pl.pallas_call(
             emit,
             out_shape=(

time: 31.7 us -> 31.6 us (level)
  no operation moved by 1% of the time
where the time goes in v5:
time: 31.6 us; the launch traced here: 31.3 us
  Pallas kernels  30.7 us (97%)
  between operations  0.64 us (2%)
    pallas_call x1, Pallas kernels, local(): pl.pallas_call(functools.partial(kernel, n_space, n_level, width, rows, b...  29.2 us
    pallas_call x1, Pallas kernels, local(): pl.pallas_call(emit, out_shape=(jax.ShapeDtypeStruct(velocity.shape, f32)...  1.51 us

profile of v5, /device:TPU:0, one launch (start us, length us, event | category | flops | bytes accessed | tf_op | source)
XLA Modules:
  0.0 31.3 jit_solution(8807981799650341602)
XLA Ops:
  0.6 29.2 %shard_map.138 = (f32[2,8,1024]{2,1,0:T(8,128)}, f32[8,1024]{1,0:T(8,128)}, f32[8,128]{1,0:T(8,128)}, f32[1,128]{1,0:T(1,128)}) custom-call(f32[2,8,1024]{2,1,0:T(8,128)} %vel.1, f32[8,1024]{1,0:T(8,128)} %den.1, f32[8,128]{1,0:T(8,128)} %bitcast.8, f32[6,2,1024]{2,1,0:T(2,128)} %bitcast.7, f32[6,1024]{1,0:T(8,128)} %lap.1, f32[8,128]{1,0:T(8,128)} %bitcast.9, ...), custom_call_target="tpu_custom_call" | custom-call | tf_op jit(solution)/shard_map/pallas_call | solution.py:432
  29.8 1.5 %shard_map.139 = (f32[2,8,1024]{2,1,0:T(8,128)}, f32[8,1024]{1,0:T(8,128)}, f32[8,128]{1,0:T(8,128)}, f32[1,4]{1,0:T(1,128)}) custom-call(f32[2,8,1024]{2,1,0:T(8,128)} %get-tuple-element.12.vel, f32[8,1024]{1,0:T(8,128)} %get-tuple-element.13.den, f32[8,128]{1,0:T(8,128)} %get-tuple-element.14.ele, f32[1,128]{1,0:T(1,128)} %get-tuple-element.15.drift), custom_call_target="tpu_custom_call" | custom-call | tf_op jit(solution)/shard_map/pallas_call | solution.py:474

commit v6 on v5

--- a/solution.py
+++ b/solution.py
@@ -42,7 +42,7 @@
     own, eta, lanes_of, block_of, east_of, north_of, smooth_of,
     flow_lanes, flow_block, flow_of, held, flow_held, press, flow, small, out, halo, halo_small, peer,
     vol, vol_line, vol_all,
-    main_send, main_recv, hs_send, hs_recv, peer_send, peer_recv, vol_send, vol_recv, column_in, load_sem, *loaded,
+    main_send, main_recv, hs_send, hs_recv, peer_send, peer_recv, vol_send, vol_recv, column_in, load_sem, vel_held, den_held, store_sem, *loaded,
 ):
     sp = lax.axis_index("space")
     lv = lax.axis_index("level")
@@ -379,21 +379,28 @@
 
     for t in range(blocks):
         here = slice(t * LANES, (t + 1) * LANES)
-        vel_out[0, :, here] = own[0, t]
-        vel_out[1, :, here] = own[1, t]
-        den_out[:, here] = own[2, t]
+        vel_held[0, :, here] = own[0, t]
+        vel_held[1, :, here] = own[1, t]
+        den_held[:, here] = own[2, t]
 
     def collect(d, total):
         q = lax.rem(sp + d, n_space)
         vol_copy(q, q).wait_recv()
         return total + vol_all[q]
 
-    total = lax.fori_loop(1, n_space, collect, vol_line[...])
+    total = collect(1, vol_line[...])
+    stores = [pltpu.make_async_copy(vel_held, vel_out, store_sem.at[0]),
+              pltpu.make_async_copy(den_held, den_out, store_sem.at[1])]
+    for store in stores:
+        store.start()
+    total = lax.fori_loop(2, n_space, collect, total)
     drifts = total / total[:, STEPS:STEPS + 1]
     shift = jnp.sum(jnp.where(lane_ids < STEPS, drifts, 0.0), axis=1, keepdims=True)
     for t in range(blocks):
         ele_out[t:t + 1, :] = eta[t][:1] + time_step * shift
     drift_out[...] = drifts
+    for store in stores:
+        store.wait()
 
     def finish(d, _):
         vol_copy(lax.rem(sp + d, n_space), sp).wait_send()
@@ -438,7 +445,7 @@
                 jax.ShapeDtypeStruct((1, LANES), f32),
             ),
             in_specs=[hbm] * 7 + [smem] + [hbm] * 3,
-            out_specs=(vmem,) * 4,
+            out_specs=(hbm, hbm, vmem, vmem),
             scratch_shapes=[
                 pltpu.VMEM((3, blocks) + tile, f32),
                 pltpu.VMEM((blocks, 8, LANES), f32),
@@ -468,6 +475,9 @@
                 dma((n_space,)), dma((n_space,)),
                 pltpu.SemaphoreType.REGULAR,
                 dma((10,)),
+                pltpu.VMEM(velocity.shape, f32),
+                pltpu.VMEM(density.shape, f32),
+                dma((2,)),
             ] + [pltpu.VMEM(a.shape, a.dtype) for a in arrays[:7] + arrays[8:]],
             compiler_params=pltpu.CompilerParams(collective_id=0, has_side_effects=True),
         )(*arrays)

time: 31.6 us -> 31.6 us (level)
  no operation moved by 1% of the time
where the time goes in v6:
time: 31.6 us; the launch traced here: 31.3 us
  Pallas kernels  30.7 us (97%)
  between operations  0.64 us (2%)
    pallas_call x1, Pallas kernels, local(): pl.pallas_call(functools.partial(kernel, n_space, n_level, width, rows, b...  29.2 us
    pallas_call x1, Pallas kernels, local(): pl.pallas_call(emit, out_shape=(jax.ShapeDtypeStruct(velocity.shape, f32)...  1.51 us

profile of v6, /device:TPU:0, one launch (start us, length us, event | category | flops | bytes accessed | tf_op | source)
XLA Modules:
  0.0 31.3 jit_solution(5203767084124319662)
XLA Ops:
  0.6 29.2 %shard_map.138 = (f32[2,8,1024]{2,1,0:T(8,128)}, f32[8,1024]{1,0:T(8,128)}, f32[8,128]{1,0:T(8,128)}, f32[1,128]{1,0:T(1,128)}) custom-call(f32[2,8,1024]{2,1,0:T(8,128)} %vel.1, f32[8,1024]{1,0:T(8,128)} %den.1, f32[8,128]{1,0:T(8,128)} %bitcast.8, f32[6,2,1024]{2,1,0:T(2,128)} %bitcast.7, f32[6,1024]{1,0:T(8,128)} %lap.1, f32[8,128]{1,0:T(8,128)} %bitcast.9, ...), custom_call_target="tpu_custom_call" | custom-call | tf_op jit(solution)/shard_map/pallas_call | solution.py:439
  29.8 1.5 %shard_map.139 = (f32[2,8,1024]{2,1,0:T(8,128)}, f32[8,1024]{1,0:T(8,128)}, f32[8,128]{1,0:T(8,128)}, f32[1,4]{1,0:T(1,128)}) custom-call(f32[2,8,1024]{2,1,0:T(8,128)} %get-tuple-element.12.vel, f32[8,1024]{1,0:T(8,128)} %get-tuple-element.13.den, f32[8,128]{1,0:T(8,128)} %get-tuple-element.14.ele, f32[1,128]{1,0:T(1,128)} %get-tuple-element.15.drift), custom_call_target="tpu_custom_call" | custom-call | tf_op jit(solution)/shard_map/pallas_call | solution.py:484
